TPU v7x, 32 devices: a whole 2x2x4 slice. The times are simulated.
32 devices in a mesh: row: 4 (over y, x), col: 8 (over z, core).
Axes of the slice: x: 2, y: 2, z: 4, core: 2. Of those that a mesh axis runs over, the one named last changes fastest.
Arguments:
- old_residual: float32 [1024, 16384], P(('row', 'col')), may hold values from -6 to 6
- group_map: int32 [32, 4], replicated, may hold values from 0 to 127, as said below
- q_factor: float32 [16384, 32], P('col', 'row'), may hold values from -0.046875 to 0.046875
Outputs:
- relaid: float32 [1024, 16384], P('row', 'col')
- projection: float32 [32, 1024], P(None, ('row', 'col'))
- row_norms: float32 [1024], P(('row', 'col'))
Inputs may be any that keep to these rules, and one draw needn't show every extreme that they name: `group_map`: all entries together are each group id 0 to 127 once; row d (old device d) holds exactly one id of each range k * 32 to (k + 1) * 32 - 1, in any slot order.
All inputs are finite; a program needn't handle non-finite values.
Results may differ from a plain program's by a relative error of at most 0.00007.
Values sent between devices are 32-bit elements; how exact they have to be, the bound alone decides.
A program may use at most 64 MiB of HBM per device.

v0:
```python
import jax
import jax.numpy as jnp
from jax import lax
from jax.sharding import PartitionSpec as P

epsilon = 1e-06


def on_device(old_residual, group_map, q_factor):
    row_count = lax.axis_size("row")
    column_count = lax.axis_size("col")
    devices_all = row_count * column_count
    my_row = lax.axis_index("row")
    my_column = lax.axis_index("col")
    position = my_row * column_count + my_column
    group_rows = old_residual.shape[0] // row_count
    full_width = old_residual.shape[1]
    block_width = full_width // column_count
    own_ids = lax.dynamic_index_in_dim(group_map, position, 0, keepdims=False)
    sending = jnp.argsort(own_ids)
    stored = jnp.take(old_residual.reshape(row_count, group_rows, full_width), sending, axis=0)
    pieces = stored.reshape(row_count, group_rows, column_count, block_width).transpose(0, 2, 1, 3)
    flat_pieces = pieces.reshape(devices_all, group_rows, block_width)
    received = lax.all_to_all(flat_pieces, ("row", "col"), split_axis=0, concat_axis=0, tiled=True)
    sorted_map = jnp.sort(group_map, axis=1)
    arriving_ids = lax.dynamic_index_in_dim(sorted_map, my_row, 1, keepdims=False)
    placement = jnp.argsort(arriving_ids)
    arranged = jnp.take(received, placement, axis=0)
    relaid_block = arranged.reshape(devices_all * group_rows, block_width)
    factor_full = lax.all_gather(q_factor, "row", axis=1, tiled=True)
    projected_share = lax.psum_scatter(
        jnp.dot(
            relaid_block,
            factor_full,
            precision=lax.Precision.HIGHEST,
            preferred_element_type=jnp.float32,
        ),
        "col",
        scatter_dimension=0,
        tiled=True,
    )
    squares = jnp.sum(relaid_block * relaid_block, axis=1)
    square_total = lax.psum_scatter(squares, "col", scatter_dimension=0, tiled=True)
    row_norms = jnp.sqrt(square_total / full_width + epsilon)
    return (relaid_block, projected_share.T, row_norms)


def solution(mesh):
    placed = (P(("row", "col"), None), P(), P("col", "row"))
    return jax.shard_map(
        on_device,
        mesh=mesh,
        in_specs=placed,
        out_specs=(P("row", "col"), P(None, ("row", "col")), P(("row", "col"))),
        check_vma=False,
    )
```

profile of v0, /device:TPU:0, one launch (start us, length us, event | category | flops | bytes accessed | tf_op | source)
XLA Modules:
  0.0 133.8 jit_solution(3552242644922017772)
XLA Ops:
  7.2 0.0 copy-start
  7.2 1.0 dynamic-slice_reduce_fusion
  8.2 0.7 sort.51
  9.0 0.0 copy-done
  9.0 2.0 %gather_fusion = f32[4,8,16384]{2,1,0:T(8,128)} fusion(f32[4,8,16384]{2,1,0:T(8,128)S(1)} %bitcast.13, s32[1024]{0:T(1024)S(1)} %pad_clamp_fusion.1), kind=kCustom, calls=%fused_computation | custom fusion | bytes 4194320 | tf_op jit(solution)/shard_map/jit(_take)/gather | solution.py:21
  11.0 3.3 %broadcast_select_fusion = f32[4,8,8,2048]{3,1,2,0:T(8,128)} fusion(f32[4,8,8,2048]{3,1,2,0:T(8,128)} %bitcast.15, pred[4]{0:T(512)(128)(4,1)S(1)} %compare_and_fusion), kind=kLoop, calls=%fused_computation.4 | loop fusion | flops 524288 | bytes 4194308 | tf_op jit(solution)/shard_map/jit(_take)/select_n | solution.py:21
  14.3 0.0 copy-start.3
  14.3 0.0 copy-start.2
  14.3 0.0 copy-start.1
  14.3 7.5 %all-to-all-start = ((f32[32,8,2048]{2,1,0:T(8,128)}), f32[32,8,2048]{2,1,0:T(8,128)}, u32[]{:S(2)}, u32[]{:S(2)}) async-start(f32[32,8,2048]{2,1,0:T(8,128)} %bitcast.14), calls=%async_computation | async-start | bytes 4194304 | tf_op jit(solution)/shard_map/all_to_all | solution.py:24
  21.7 0.0 reduce-scatter.2.cloned.1.call-start
  21.8 0.0 copy-done.3
  21.8 0.6 dynamic-slice
  23.0 0.0 copy-done.2
  23.1 0.6 sort.49
  23.7 1.6 %sort.50 = (s32[32]{0:T(128)}, s32[32]{0:T(128)S(1)}) sort(s32[32]{0:T(128)S(1)} %dynamic-slice_bitcast_fusion, s32[32]{0:T(128)S(1)} %iota.12), dimensions={0}, to_apply=%region_1.2 | sort | flops 160 | bytes 512 | tf_op jit(solution)/shard_map/jit(argsort)/sort | solution.py:27
  25.3 0.1 broadcast_in_dim.32
  25.4 0.1 broadcast_in_dim.33
  25.5 0.0 copy-done.1
  25.5 16.7 %all_gather.3 = f32[2048,32]{0,1:T(8,128)S(1)} all-gather(f32[2048,8]{0,1:T(8,128)S(1)} %copy-done.1), channel_id=1, replica_groups=mesh['row'=4,'col'=8] {'row'}, dimensions={1}, use_global_device_ids=true | all-gather | bytes 327680 | tf_op jit(solution)/shard_map/all_gather | solution.py:30
  42.2 29.5 %all-to-all-done = f32[32,8,2048]{2,1,0:T(8,128)} async-done(((f32[32,8,2048]{2,1,0:T(8,128)}), f32[32,8,2048]{2,1,0:T(8,128)}, u32[]{:S(2)}, u32[]{:S(2)}) %all-to-all-start) | async-done | bytes 2097184 | tf_op jit(solution)/shard_map/all_to_all | solution.py:24
  71.7 3.6 %gather_fusion.1 = f32[32,8,2048]{2,1,0:T(8,128)} fusion(f32[32,8,2048]{2,1,0:T(8,128)} %all-to-all-done, s32[1024]{0:T(1024)S(1)} %pad_clamp_fusion), kind=kCustom, calls=%fused_computation.1 | custom fusion | bytes 4194432 | tf_op jit(solution)/shard_map/jit(_take)/gather | solution.py:28
  75.3 1.9 %multiply_reduce_fusion = f32[32,8]{1,0:T(8,128)S(1)} fusion(f32[32,8,2048]{2,1,0:T(8,128)} %gather_fusion.1, pred[32]{0:T(512)(128)(4,1)S(1)} %compare_and_fusion.1), kind=kLoop, calls=%fused_computation.3 | loop fusion | flops 1572608 | bytes 2098208 | tf_op jit(solution)/shard_map/reduce_sum | solution.py:42
  77.2 0.1 reduce_sum.12
  77.3 3.1 %bitcast_select_fusion = f32[256,2048]{1,0:T(8,128)} fusion(f32[32,8,2048]{2,1,0:T(8,128)} %gather_fusion.1, pred[256]{0:T(512)(128)(4,1)S(1)} %broadcast_in_dim.33), kind=kLoop, calls=%fused_computation.2 | loop fusion | flops 524288 | bytes 4194560 | tf_op jit(solution)/shard_map/jit(_take)/select_n | solution.py:28
  80.5 13.6 %all-reduce = f32[256]{0:T(256)S(1)} all-reduce(f32[256]{0:T(256)S(1)} %reduce_sum.12), channel_id=3, replica_groups=mesh['row'=4,'col'=8] {'col'}, use_global_device_ids=true, to_apply=%region_5.6.clone | all-reduce | flops 256 | bytes 2048
  94.0 4.0 %fusion.2 = f32[256,32]{1,0:T(8,128)} fusion(f32[256,2048]{1,0:T(8,128)} %bitcast_select_fusion, f32[2048,32]{0,1:T(8,128)S(1)} %all_gather.3), kind=kOutput, calls=%fused_computation.16 | convolution fusion | flops 201326592 | bytes 2392064 | tf_op jit(solution)/shard_map/dot_general | solution.py:32
  98.0 0.0 reduce-scatter.2.cloned.1.call-update
  98.1 0.6 fusion.1
  98.7 26.9 %reduce-scatter.2.cloned.1.call-done = f32[32,32]{1,0:T(8,128)} async-done(((f32[256,32]{1,0:T(8,128)}), f32[32,32]{1,0:T(8,128)}) %reduce-scatter.2.cloned.1.call-update) | async-done | bytes 4112 | tf_op jit(solution)/shard_map/reduce_scatter | solution.py:31
  125.5 1.4 %copy.8 = f32[32,32]{1,0:T(8,128)} copy(f32[32,32]{0,1:T(8,128)} %bitcast.16) | data formatting | bytes 8192
  (10 shorter events, 0.0 us)
Async XLA Ops:
  7.2 1.8 %copy-start = (f32[32,16384]{1,0:T(8,128)S(1)}, f32[32,16384]{1,0:T(8,128)}, u32[]{:S(2)}) copy-start(f32[32,16384]{1,0:T(8,128)} %param.3) | copy-start | bytes 6291460
  14.3 7.5 %copy-start.3 = (u32[32]{0:T(128)S(1)}, u32[32]{0:T(128)}, u32[]{:S(2)}) copy-start(u32[32]{0:T(128)} %constant.57) | copy-start | bytes 388
  14.3 8.8 %copy-start.2 = (s32[32,4]{0,1:T(4,128)S(1)}, s32[32,4]{0,1:T(4,128)}, u32[]{:S(2)}) copy-start(s32[32,4]{0,1:T(4,128)} %param.4) | copy-start | bytes 1540
  14.3 11.2 %copy-start.1 = (f32[2048,8]{0,1:T(8,128)S(1)}, f32[2048,8]{0,1:T(8,128)}, u32[]{:S(2)}) copy-start(f32[2048,8]{0,1:T(8,128)} %param.5) | copy-start | bytes 196612
  14.3 57.5 %all-to-all-start = ((f32[32,8,2048]{2,1,0:T(8,128)}), f32[32,8,2048]{2,1,0:T(8,128)}, u32[]{:S(2)}, u32[]{:S(2)}) async-start(f32[32,8,2048]{2,1,0:T(8,128)} %bitcast.14), calls=%async_computation | async-start | bytes 4194304 | tf_op jit(solution)/shard_map/all_to_all | solution.py:24
  21.7 103.8 %reduce-scatter.2.cloned.1.call-start = ((), (), s32[]{:S(2)}) async-start(), calls=%async_computation.2 | async-start | bytes 147456 | tf_op jit(solution)/shard_map/reduce_scatter | solution.py:31
Sparse Core Ops, SparseCore 0:
  98.2 27.3 reduce-scatter.1
where the time goes:
time: 134 us
  waiting for transfers between devices  56.4 us (42%)
  blocking collectives  30.3 us (23%)
  between operations  14.8 us (11%)
  other arithmetic  11.9 us (9%)
  local copies, waits for them, and re-layouts  8.86 us (7%)
  starting transfers between devices  7.5 us (6%)
  matrix products  3.99 us (3%)
    all_to_all x1, waiting for transfers between devices, on_device(): lax.all_to_all(flat_pieces, ('row', 'col'), split_axis=0, concat_axis=0,...  29.5 us
    reduce_scatter x1, waiting for transfers between devices, on_device(): lax.psum_scatter(jnp.dot(relaid_block, factor_full, precision=lax.Precisi...  26.9 us
    all_gather x1, blocking collectives, on_device(): factor_full = lax.all_gather(q_factor, 'row', axis=1, tiled=True)  16.7 us
    unnamed x1, blocking collectives  13.6 us
    all_to_all x1, starting transfers between devices, on_device(): lax.all_to_all(flat_pieces, ('row', 'col'), split_axis=0, concat_axis=0,...  7.45 us
    dot_general x1, matrix products, on_device(): jnp.dot(relaid_block, factor_full, precision=lax.Precision.HIGHEST, prefe...  3.99 us
    gather x1, local copies, waits for them, and re-layouts, on_device(): arranged = jnp.take(received, placement, axis=0)  3.56 us
    select_n x2, other arithmetic, on_device(): jnp.take(old_residual.reshape(row_count, group_rows, full_width), sending...  3.28 us
  transfers between devices with their start and end apart: 2, of which 2 were waited for; matrix products, arithmetic and copies ran while one was open for 3% of the time, Pallas kernels for 0%

commit v1 on v0

--- a/solution.py
+++ b/solution.py
@@ -27,7 +27,8 @@
     placement = jnp.argsort(arriving_ids)
     arranged = jnp.take(received, placement, axis=0)
     relaid_block = arranged.reshape(devices_all * group_rows, block_width)
-    factor_full = lax.all_gather(q_factor, "row", axis=1, tiled=True)
+    parts = lax.all_gather(q_factor, "row", axis=0, tiled=False)
+    factor_full = jnp.concatenate(parts, axis=1)
     projected_share = lax.psum_scatter(
         jnp.dot(
             relaid_block,

time: 134 us -> 117 us (0.87)
  waiting for transfers between devices: 56.4 us -> 40.5 us
  matrix products: 3.99 us -> 2.49 us
    reduce_scatter x1, waiting for transfers between devices: 26.9 us -> 11 us  [on_device(): lax.psum_scatter(jnp.dot(relaid_block, factor_full, precision=lax.Precisi...]
    dot_general x1, matrix products: 3.99 us -> 2.49 us  [on_device(): jnp.dot(relaid_block, factor_full, precision=lax.Precision.HIGHEST, prefe...]
  transfers between devices with their start and end apart: 2 -> 2, of which waited for: 2 -> 2; matrix products, arithmetic and copies ran while one was open for 3% -> 6% of each run, Pallas kernels for 0% -> 0%
where the time goes in v1:
time: 117 us
  waiting for transfers between devices  40.5 us (35%)
  blocking collectives  30.4 us (26%)
  between operations  14.8 us (13%)
  other arithmetic  12.1 us (10%)
  local copies, waits for them, and re-layouts  9.04 us (8%)
  starting transfers between devices  7.5 us (6%)
  matrix products  2.49 us (2%)
    all_to_all x1, waiting for transfers between devices, on_device(): lax.all_to_all(flat_pieces, ('row', 'col'), split_axis=0, concat_axis=0,...  29.5 us
    all_gather x1, blocking collectives, on_device(): parts = lax.all_gather(q_factor, 'row', axis=0, tiled=False)  16.7 us
    unnamed x1, blocking collectives  13.6 us
    reduce_scatter x1, waiting for transfers between devices, on_device(): lax.psum_scatter(jnp.dot(relaid_block, factor_full, precision=lax.Precisi...  11 us
    all_to_all x1, starting transfers between devices, on_device(): lax.all_to_all(flat_pieces, ('row', 'col'), split_axis=0, concat_axis=0,...  7.45 us
    gather x1, local copies, waits for them, and re-layouts, on_device(): arranged = jnp.take(received, placement, axis=0)  3.62 us
    select_n x2, other arithmetic, on_device(): jnp.take(old_residual.reshape(row_count, group_rows, full_width), sending...  3.28 us
    select_n x2, other arithmetic, on_device(): arranged = jnp.take(received, placement, axis=0)  3.12 us
  transfers between devices with their start and end apart: 2, of which 2 were waited for; matrix products, arithmetic and copies ran while one was open for 6% of the time, Pallas kernels for 0%

profile of v1, /device:TPU:0, one launch (start us, length us, event | category | flops | bytes accessed | tf_op | source)
XLA Modules:
  0.0 116.7 jit_solution(15376447841465269885)
XLA Ops:
  7.2 0.0 copy-start
  7.2 1.0 dynamic-slice_reduce_fusion
  8.2 0.7 sort.51
  9.0 0.0 copy-done
  9.0 2.0 %gather_fusion = f32[4,8,16384]{2,1,0:T(8,128)} fusion(f32[4,8,16384]{2,1,0:T(8,128)S(1)} %bitcast.20, s32[1024]{0:T(1024)S(1)} %pad_clamp_fusion.1), kind=kCustom, calls=%fused_computation | custom fusion | bytes 4194320 | tf_op jit(solution)/shard_map/jit(_take)/gather | solution.py:21
  11.0 3.3 %broadcast_select_fusion = f32[4,8,8,2048]{3,1,2,0:T(8,128)} fusion(f32[4,8,8,2048]{3,1,2,0:T(8,128)} %bitcast.22, pred[4]{0:T(512)(128)(4,1)S(1)} %compare_and_fusion), kind=kLoop, calls=%fused_computation.8 | loop fusion | flops 524288 | bytes 4194308 | tf_op jit(solution)/shard_map/jit(_take)/select_n | solution.py:21
  14.3 0.0 copy-start.4
  14.3 0.0 copy-start.3
  14.3 0.0 copy-start.2
  14.3 7.5 %all-to-all-start = ((f32[32,8,2048]{2,1,0:T(8,128)}), f32[32,8,2048]{2,1,0:T(8,128)}, u32[]{:S(2)}, u32[]{:S(2)}) async-start(f32[32,8,2048]{2,1,0:T(8,128)} %bitcast.21), calls=%async_computation | async-start | bytes 4194304 | tf_op jit(solution)/shard_map/all_to_all | solution.py:24
  21.7 0.0 reduce-scatter.2.cloned.1.call-start
  21.8 0.0 copy-done.4
  21.8 0.6 dynamic-slice
  23.0 0.0 copy-done.3
  23.1 0.6 sort.49
  23.7 1.6 %sort.50 = (s32[32]{0:T(128)}, s32[32]{0:T(128)S(1)}) sort(s32[32]{0:T(128)S(1)} %dynamic-slice_bitcast_fusion, s32[32]{0:T(128)S(1)} %iota.12), dimensions={0}, to_apply=%region_1.2 | sort | flops 160 | bytes 512 | tf_op jit(solution)/shard_map/jit(argsort)/sort | solution.py:27
  25.3 0.1 broadcast_in_dim.32
  25.4 0.1 broadcast_in_dim.33
  25.5 0.0 copy-done.2
  25.5 16.7 %all-gather = f32[8192,8]{0,1:T(8,128)S(1)} all-gather(f32[2048,8]{0,1:T(8,128)S(1)} %copy-done.2), channel_id=2, replica_groups=mesh['row'=4,'col'=8] {'row'}, dimensions={0}, use_global_device_ids=true | all-gather | bytes 327680 | tf_op jit(solution)/shard_map/all_gather | solution.py:30
  42.2 29.5 %all-to-all-done = f32[32,8,2048]{2,1,0:T(8,128)} async-done(((f32[32,8,2048]{2,1,0:T(8,128)}), f32[32,8,2048]{2,1,0:T(8,128)}, u32[]{:S(2)}, u32[]{:S(2)}) %all-to-all-start) | async-done | bytes 2097184 | tf_op jit(solution)/shard_map/all_to_all | solution.py:24
  71.7 3.6 %gather_fusion.1 = f32[32,8,2048]{2,1,0:T(8,128)} fusion(f32[32,8,2048]{2,1,0:T(8,128)} %all-to-all-done, s32[1024]{0:T(1024)S(1)} %pad_clamp_fusion), kind=kCustom, calls=%fused_computation.1 | custom fusion | bytes 4194432 | tf_op jit(solution)/shard_map/jit(_take)/gather | solution.py:28
  75.4 0.0 copy-start.1
  75.4 2.1 %multiply_reduce_fusion = f32[32,8]{1,0:T(8,128)S(1)} fusion(f32[32,8,2048]{2,1,0:T(8,128)} %gather_fusion.1, pred[32]{0:T(512)(128)(4,1)S(1)} %compare_and_fusion.1), kind=kLoop, calls=%fused_computation.5 | loop fusion | flops 1572608 | bytes 2098208 | tf_op jit(solution)/shard_map/reduce_sum | solution.py:43
  77.5 0.1 copy-done.1
  77.6 2.5 %fusion = f32[256,32]{1,0:T(8,128)} fusion(f32[2048,32]{0,1:T(8,128)S(1)} %bitcast.23, f32[32,8,2048]{2,1,0:T(8,128)S(1)} %copy-done.1, pred[32]{0:T(512)(128)(4,1)S(1)} %compare_and_fusion.1), kind=kOutput, calls=%fused_computation.2 | convolution fusion | flops 201850880 | bytes 2392096 | tf_op jit(solution)/shard_map/dot_general | solution.py:33
  80.1 0.0 reduce-scatter.2.cloned.1.call-update
  80.1 0.1 reduce_sum.12
  80.2 3.1 %bitcast_select_fusion = f32[256,2048]{1,0:T(8,128)} fusion(f32[32,8,2048]{2,1,0:T(8,128)} %gather_fusion.1, pred[256]{0:T(512)(128)(4,1)S(1)} %broadcast_in_dim.33), kind=kLoop, calls=%fused_computation.4 | loop fusion | flops 524288 | bytes 4194560 | tf_op jit(solution)/shard_map/jit(_take)/select_n | solution.py:28
  83.3 13.6 %all-reduce = f32[256]{0:T(256)S(1)} all-reduce(f32[256]{0:T(256)S(1)} %reduce_sum.12), channel_id=4, replica_groups=mesh['row'=4,'col'=8] {'col'}, use_global_device_ids=true, to_apply=%region_5.6.clone | all-reduce | flops 256 | bytes 2048
  96.9 0.6 fusion.6
  97.5 11.0 %reduce-scatter.2.cloned.1.call-done = f32[32,32]{1,0:T(8,128)} async-done(((f32[256,32]{1,0:T(8,128)}), f32[32,32]{1,0:T(8,128)}) %reduce-scatter.2.cloned.1.call-update) | async-done | bytes 4112 | tf_op jit(solution)/shard_map/reduce_scatter | solution.py:32
  108.5 1.4 %copy.8 = f32[32,32]{1,0:T(8,128)} copy(f32[32,32]{0,1:T(8,128)} %bitcast.24) | data formatting | bytes 8192
  (10 shorter events, 0.0 us)
Async XLA Ops:
  7.2 1.8 %copy-start = (f32[32,16384]{1,0:T(8,128)S(1)}, f32[32,16384]{1,0:T(8,128)}, u32[]{:S(2)}) copy-start(f32[32,16384]{1,0:T(8,128)} %param.3) | copy-start | bytes 6291460
  14.3 7.5 %copy-start.4 = (u32[32]{0:T(128)S(1)}, u32[32]{0:T(128)}, u32[]{:S(2)}) copy-start(u32[32]{0:T(128)} %constant.57) | copy-start | bytes 388
  14.3 8.8 %copy-start.3 = (s32[32,4]{0,1:T(4,128)S(1)}, s32[32,4]{0,1:T(4,128)}, u32[]{:S(2)}) copy-start(s32[32,4]{0,1:T(4,128)} %param.4) | copy-start | bytes 1540
  14.3 11.2 %copy-start.2 = (f32[2048,8]{0,1:T(8,128)S(1)}, f32[2048,8]{0,1:T(8,128)}, u32[]{:S(2)}) copy-start(f32[2048,8]{0,1:T(8,128)} %param.5) | copy-start | bytes 196612
  14.3 57.5 %all-to-all-start = ((f32[32,8,2048]{2,1,0:T(8,128)}), f32[32,8,2048]{2,1,0:T(8,128)}, u32[]{:S(2)}, u32[]{:S(2)}) async-start(f32[32,8,2048]{2,1,0:T(8,128)} %bitcast.21), calls=%async_computation | async-start | bytes 4194304 | tf_op jit(solution)/shard_map/all_to_all | solution.py:24
  21.7 86.8 %reduce-scatter.2.cloned.1.call-start = ((), (), s32[]{:S(2)}) async-start(), calls=%async_computation.2 | async-start | bytes 147456 | tf_op jit(solution)/shard_map/reduce_scatter | solution.py:32
  75.4 2.2 %copy-start.1 = (f32[32,8,2048]{2,1,0:T(8,128)S(1)}, f32[32,8,2048]{2,1,0:T(8,128)}, u32[]{:S(2)}) copy-start(f32[32,8,2048]{2,1,0:T(8,128)} %gather_fusion.1) | copy-start | bytes 6291460
Sparse Core Ops, SparseCore 0:
  80.2 28.2 reduce-scatter.1
